TPU v7x, 128 devices: a whole 4x4x4 slice. The times are simulated.
128 devices in a mesh: gx: 8 (over z, core), gy: 16 (over x, y).
Axes of the slice: x: 4, y: 4, z: 4, core: 2. Of those that a mesh axis runs over, the one named last changes fastest.
Arguments:
- policy_logp: float32 [16, 2048, 4096], P('gy', 'gx'), may hold values from -2 to 0
- anchor_logp: float32 [16, 2048, 4096], P('gy', 'gx'), may hold values from -2 to 0
- lengths: int32 [16, 2048], P('gy', 'gx'), may hold values from 512 to 4096
- rewards: int32 [16, 2048], P('gy', 'gx'), may hold values from 0 to 8
- slot_prompt: int32 [16, 2048], P('gy', 'gx'), may hold values from 0 to 2047, as said below
Outputs:
- token_grad: float32 [16, 2048, 4096], P(None, ('gx', 'gy'))
- sample_loss: float32 [16, 2048], P(None, ('gx', 'gy'))
- advantage: float32 [16, 2048], P(None, ('gx', 'gy'))
Inputs may be any that keep to these rules, and one draw needn't show every extreme that they name: `slot_prompt`: for every member k and every aligned block of 256 slots, the slots of the block hold each prompt of the same block exactly once.
All inputs are finite; a program needn't handle non-finite values.
Results may differ from a plain program's by a relative error of at most 0.00002.
Values sent between devices are 32-bit elements; how exact they have to be, the bound alone decides.
A program may use at most 64 MiB of HBM per device.

v0:
```python
import jax
import jax.numpy as jnp
from jax import lax
from jax.sharding import Mesh
from jax.sharding import PartitionSpec as P

GX_GY = ("gx_0", "gx_1", "gy_0", "gy_1")
GY = ("gy_0", "gy_1")
GX = ("gx_0", "gx_1")
kl_weight = 0.1


def by_axis(x, axes):
    for axis in axes:
        x = lax.psum(x, axis)
    return x


def sent_together(arrays, axis, split_dim, concat_dim, along):
    columns = [a.reshape(*a.shape[:along], -1) for a in arrays]
    both = jnp.concatenate(columns, axis=along)
    out, at, gathered = (
        lax.all_to_all(both, axis, split_axis=split_dim, concat_axis=concat_dim, tiled=True),
        0,
        [],
    )
    for a, column in zip(arrays, columns):
        piece = out[..., at : at + column.shape[along]]
        gathered.append(piece.reshape(*piece.shape[:along], *a.shape[along:]))
        at += column.shape[along]
    return tuple(gathered)


def score_tokens(policy, anchor, seq_len, reward, total, members, grad_scale, loss_scale):
    advantage = (members * reward - total[None, :]) / (members - 1)
    positions = lax.broadcasted_iota(jnp.float32, policy.shape, 2)
    valid = positions < seq_len[:, :, None]
    log_ratio = anchor - policy
    ratio = jnp.exp(log_ratio)
    token_term = -advantage[:, :, None] * policy + kl_weight * (ratio - log_ratio - 1.0)
    token_grad = (
        jnp.where(valid, -advantage[:, :, None] + kl_weight * (1.0 - ratio), 0.0) * grad_scale
    )
    sample_loss = jnp.sum(jnp.where(valid, token_term, 0.0), axis=2) * loss_scale
    return (token_grad, sample_loss, advantage)


def body(policy_logp, anchor_logp, lengths, rewards, slot_prompt):
    members_dev, slots, seq_slots = policy_logp.shape
    local_prompt = slot_prompt % slots
    member_rows = lax.broadcasted_iota(jnp.int32, (members_dev, slots), 0)
    slot_ids = lax.broadcasted_iota(jnp.int32, (members_dev, slots), 1)
    inverse = jnp.zeros((members_dev, slots), jnp.int32).at[member_rows, local_prompt].set(slot_ids)
    sorted_policy = jnp.take_along_axis(policy_logp, inverse[:, :, None], axis=1)
    sorted_anchor = jnp.take_along_axis(anchor_logp, inverse[:, :, None], axis=1)
    sorted_len = jnp.take_along_axis(lengths, inverse, axis=1).astype(jnp.float32)
    sorted_reward = jnp.take_along_axis(rewards, inverse, axis=1).astype(jnp.float32) * 0.25
    count_local = jnp.sum(lengths.astype(jnp.float32))
    token_total = by_axis(count_local, GX_GY)
    members = members_dev * lax.axis_size(GY)
    samples = members * slots * lax.axis_size(GX)
    grad_scale = samples * seq_slots / token_total
    loss_scale = samples / token_total
    member_sums = jnp.sum(sorted_reward, axis=0)
    total = by_axis(member_sums, GY)
    token_grad, sample_loss, advantage = score_tokens(
        sorted_policy,
        sorted_anchor,
        sorted_len,
        sorted_reward,
        total,
        members,
        grad_scale,
        loss_scale,
    )
    return sent_together((token_grad, sample_loss, advantage), GY, 1, 0, 2)


def solution(mesh):
    torus = Mesh(mesh.devices.reshape(4, 2, 4, 4), ("gx_0", "gx_1", "gy_0", "gy_1"))
    return jax.shard_map(
        body,
        mesh=torus,
        in_specs=(P(GY, GX, None), P(GY, GX, None), P(GY, GX), P(GY, GX), P(GY, GX)),
        out_specs=(P(None, GX_GY, None), P(None, GX_GY), P(None, GX_GY)),
        check_vma=False,
    )
```

profile of v0, /device:TPU:0, one launch (start us, length us, event | category | flops | bytes accessed | tf_op | source)
XLA Modules:
  0.0 137.0 jit_solution(9556072892073195460)
XLA Ops:
  0.6 0.0 copy-start
  0.6 1.3 convert_reduce_fusion
  1.9 12.5 %psum.44 = f32[]{:T(128)} all-reduce(f32[]{:T(128)} %convert_reduce_fusion), channel_id=1, replica_groups=mesh['gx_0'=4,'gx_1'=2,'gy_0'=4,'gy_1'=4] {'gx_0'}, use_global_device_ids=true, to_apply=%region_4.7 | all-reduce | flops 1 | bytes 8 | tf_op jit(solution)/shard_map/psum | solution.py:15
  14.4 3.1 %psum.45 = f32[]{:T(128)} all-reduce(f32[]{:T(128)} %psum.44), channel_id=1, replica_groups=mesh['gx_0'=4,'gx_1'=2,'gy_0'=4,'gy_1'=4] {'gx_1'}, use_global_device_ids=true, to_apply=%region_5.8 | all-reduce | flops 1 | bytes 8 | tf_op jit(solution)/shard_map/psum | solution.py:15
  17.5 0.7 fusion.11
  18.2 1.4 %scatter_custom_fusion = s32[256]{0:T(256)S(1)} fusion(s32[256]{0:T(256)S(1)} %bitcast.61, s32[256]{0:T(256)S(1)} %iota.12, s32[]{:T(128)} %constant.18.clone.1), kind=kCustom, calls=%fused_computation.40 | custom fusion | bytes 1028 | tf_op jit(solution)/shard_map/scatter | solution.py:53
  19.7 0.0 copy-done
  19.7 1.9 %gather_fusion.1 = s32[256]{0:T(256)S(1)} fusion(s32[256]{0:T(256)S(1)} %bitcast.41, s32[1024]{0:T(1024)S(1)} %pad_clamp_fusion.1), kind=kCustom, calls=%fused_computation.2.clone | custom fusion | bytes 3072 | tf_op jit(solution)/shard_map/jit(take_along_axis)/gather | solution.py:57
  21.7 2.0 %gather_fusion = s32[256]{0:T(256)S(1)} fusion(s32[256]{0:T(256)} %bitcast.42, s32[1024]{0:T(1024)S(1)} %pad_clamp_fusion.1), kind=kCustom, calls=%fused_computation.clone | custom fusion | bytes 3072 | tf_op jit(solution)/shard_map/jit(take_along_axis)/gather | solution.py:56
  23.7 11.1 %all-reduce.2 = (f32[]{:T(128)}, f32[256]{0:T(256)S(1)}) all-reduce(f32[]{:T(128)} %psum.45, f32[256]{0:T(256)S(1)} %bitcast.62), channel_id=1, replica_groups=mesh['gx_0'=4,'gx_1'=2,'gy_0'=4,'gy_1'=4] {'gy_0'}, use_global_device_ids=true, to_apply=%region_6.9 | all-reduce | flops 257 | bytes 2056 | tf_op jit(solution)/shard_map/psum | solution.py:15
  34.8 11.3 %all-reduce.1 = (f32[]{:T(128)}, f32[1,256]{1,0:T(1,128)S(1)}) all-reduce(f32[]{:T(128)} %get-tuple-element.9, f32[1,256]{1,0:T(1,128)S(1)} %bitcast.63), channel_id=1, replica_groups=mesh['gx_0'=4,'gx_1'=2,'gy_0'=4,'gy_1'=4] {'gy_1'}, use_global_device_ids=true, to_apply=%region_7.10 | all-reduce | flops 257 | bytes 2056 | tf_op jit(solution)/shard_map/psum | solution.py:15
  47.5 0.1 copy.23
  47.7 7.9 %gather_fusion.3 = f32[256,4096]{1,0:T(8,128)} fusion(f32[256,4096]{1,0:T(8,128)} %bitcast.43, s32[1024]{0:T(1024)S(1)} %pad_clamp_fusion), kind=kCustom, calls=%fused_computation.3.clone | custom fusion | bytes 8389632 | tf_op jit(solution)/shard_map/jit(take_along_axis)/gather | solution.py:54
  55.6 7.8 %gather_fusion.2 = f32[256,4096]{1,0:T(8,128)} fusion(f32[256,4096]{1,0:T(8,128)} %bitcast.44, s32[1024]{0:T(1024)S(1)} %pad_clamp_fusion), kind=kCustom, calls=%fused_computation.1.clone | custom fusion | bytes 8389632 | tf_op jit(solution)/shard_map/jit(take_along_axis)/gather | solution.py:55
  63.4 6.4 %fusion.8 = (f32[256]{0:T(256)S(1)}, f32[1,256,4096]{2,1,0:T(8,128)}) fusion(f32[256,4096]{1,0:T(8,128)} %gather_fusion.3, f32[256,4096]{1,0:T(8,128)} %gather_fusion.2, f32[256]{0:T(256)S(1)} %bitcast.55, f32[256]{0:T(256)S(1)} %bitcast.54, pred[256]{0:T(512)(128)(4,1)S(1)} %get-tuple-element.11, f32[]{:T(128)S(6)} %div.14), kind=kLoop, calls=%fused_computation.15 | loop fusion | flops 16776960 | bytes 12586244 | tf_op jit(solution)/shard_map/reduce_sum | solution.py:44
  69.7 0.1 copy.22
  69.9 5.6 %concatenate.7 = f32[1,256,4098]{2,1,0:T(8,128)} concatenate(f32[1,256,4096]{2,1,0:T(8,128)} %get-tuple-element.16, f32[1,256,1]{2,1,0:T(8,128)S(1)} %copy.22, f32[1,256,1]{2,1,0:T(8,128)S(1)} %copy.23), dimensions={2} | concatenate | bytes 8392704 | tf_op jit(solution)/shard_map/concatenate | solution.py:21
  75.5 6.7 %copy.24 = f32[1,256,4098]{2,0,1:T(1,128)S(1)} copy(f32[1,256,4098]{2,1,0:T(8,128)} %concatenate.7) | data formatting | bytes 8392704 | tf_op jit(solution)/shard_map/concatenate | solution.py:21
  82.1 51.2 %all_to_all.12 = f32[1,256,4098]{2,0,1:T(1,128)S(1)} all-to-all(f32[1,256,4098]{2,0,1:T(1,128)S(1)} %copy.24), channel_id=1, replica_groups=mesh['gx_0'=4,'gx_1'=2,'gy_0'=4,'gy_1'=4] {'gy_0','gy_1'}, dimensions={1} | all-to-all | bytes 8392704 | tf_op jit(solution)/shard_map/all_to_all | solution.py:23
  133.4 0.3 copy.25
  133.7 0.8 slice_reduce_fusion
  134.5 2.5 %slice.24 = f32[16,16,4096]{2,1,0:T(8,128)} slice(f32[16,16,4098]{2,1,0:T(8,128)S(1)} %bitcast.46), slice={[0:16], [0:16], [0:4096]} | slice | bytes 8388608 | tf_op jit(solution)/shard_map/slice | solution.py:28
  (11 shorter events, 0.1 us)
Async XLA Ops:
  0.6 19.1 %copy-start = (s32[1,256]{1,0:T(1,128)S(1)}, s32[1,256]{1,0:T(1,128)}, u32[]{:S(2)}) copy-start(s32[1,256]{1,0:T(1,128)} %param.12) | copy-start | bytes 3076
where the time goes:
time: 138 us; the launch traced here: 137 us
  blocking collectives  89.3 us (65%)
  local copies, waits for them, and re-layouts  37.2 us (27%)
  other arithmetic  8.42 us (6%)
  between operations  2.11 us (2%)
    all_to_all x1, blocking collectives, sent_together(): lax.all_to_all(both, axis, split_axis=split_dim, concat_axis=concat_dim,...  51.2 us
    psum x4, blocking collectives, by_axis(): x = lax.psum(x, axis)  38 us
    concatenate x2, local copies, waits for them, and re-layouts, sent_together(): both = jnp.concatenate(columns, axis=along)  12.2 us
    gather x1, local copies, waits for them, and re-layouts, body(): jnp.take_along_axis(policy_logp, inverse[:, :, None], axis=1)  7.89 us
    gather x1, local copies, waits for them, and re-layouts, body(): jnp.take_along_axis(anchor_logp, inverse[:, :, None], axis=1)  7.8 us
    reduce_sum x1, other arithmetic, score_tokens(): jnp.sum(jnp.where(valid, token_term, 0.0), axis=2) * loss_scale  6.36 us
    slice x2, local copies, waits for them, and re-layouts, sent_together(): piece = out[..., at:at + column.shape[along]]  3.33 us

commit v1 on v0

--- a/solution.py
+++ b/solution.py
@@ -3,6 +3,7 @@
 from jax import lax
 from jax.sharding import Mesh
 from jax.sharding import PartitionSpec as P
+from jax.lax import all_gather
 
 GX_GY = ("gx_0", "gx_1", "gy_0", "gy_1")
 GY = ("gy_0", "gy_1")
@@ -12,7 +13,7 @@
 
 def by_axis(x, axes):
     for axis in axes:
-        x = lax.psum(x, axis)
+        x = jnp.sum(all_gather(x, axis), axis=0)
     return x
 
 

time: 138 us -> 160 us (1.16)
  local copies, waits for them, and re-layouts: 37.2 us -> 47.7 us
  blocking collectives: 89.3 us -> 98.4 us
  other arithmetic: 8.42 us -> 10.9 us
    psum x4 -> x0, blocking collectives: 38 us -> none  [by_axis(): x = lax.psum(x, axis)]
    unnamed x0 -> x4, blocking collectives: none -> 35.5 us
    all_gather x0 -> x2, blocking collectives: none -> 14 us  [by_axis(): x = jnp.sum(all_gather(x, axis), axis=0)]
    unnamed x3 -> x15, local copies, waits for them, and re-layouts: 0.29 us -> 10.8 us
    reduce_sum x0 -> x6, other arithmetic: none -> 2.46 us  [by_axis(): x = jnp.sum(all_gather(x, axis), axis=0)]
    all_to_all x1, blocking collectives: 51.2 us -> 49 us  [sent_together(): lax.all_to_all(both, axis, split_axis=split_dim, concat_axis=concat_dim,...]
where the time goes in v1:
time: 160 us; the launch traced here: 159 us
  blocking collectives  98.4 us (62%)
  local copies, waits for them, and re-layouts  47.7 us (30%)
  other arithmetic  10.9 us (7%)
  between operations  2.13 us (1%)
    all_to_all x1, blocking collectives, sent_together(): lax.all_to_all(both, axis, split_axis=split_dim, concat_axis=concat_dim,...  49 us
    unnamed x4, blocking collectives  35.5 us
    all_gather x2, blocking collectives, by_axis(): x = jnp.sum(all_gather(x, axis), axis=0)  14 us
    concatenate x2, local copies, waits for them, and re-layouts, sent_together(): both = jnp.concatenate(columns, axis=along)  12.2 us
    unnamed x15, local copies, waits for them, and re-layouts  10.8 us
    gather x1, local copies, waits for them, and re-layouts, body(): jnp.take_along_axis(policy_logp, inverse[:, :, None], axis=1)  7.89 us
    gather x1, local copies, waits for them, and re-layouts, body(): jnp.take_along_axis(anchor_logp, inverse[:, :, None], axis=1)  7.8 us
    reduce_sum x1, other arithmetic, score_tokens(): jnp.sum(jnp.where(valid, token_term, 0.0), axis=2) * loss_scale  6.36 us

profile of v1, /device:TPU:0, one launch (start us, length us, event | category | flops | bytes accessed | tf_op | source)
XLA Modules:
  0.0 159.2 jit_solution(11853387283083455092)
XLA Ops:
  0.6 0.0 copy-start
  0.7 1.3 convert_reduce_fusion
  1.9 1.2 dynamic-slice
  3.2 1.4 dynamic-update-slice
  4.6 1.2 dynamic-slice.1
  5.8 11.8 %all-reduce.1 = f32[4]{0:T(128)S(1)} all-reduce(f32[4]{0:T(128)S(1)} %dynamic-update-slice), channel_id=1, replica_groups=mesh['gx_0'=4,'gx_1'=2,'gy_0'=4,'gy_1'=4] {'gx_0'}, use_global_device_ids=true, to_apply=%add.1 | all-reduce | flops 4 | bytes 32
  17.7 0.6 reduce_sum.79
  18.3 1.4 dynamic-update-slice.1
  19.7 1.2 dynamic-slice.2
  20.9 2.4 %all-reduce.2 = f32[2]{0:T(128)S(1)} all-reduce(f32[2]{0:T(128)S(1)} %dynamic-update-slice.1), channel_id=1, replica_groups=mesh['gx_0'=4,'gx_1'=2,'gy_0'=4,'gy_1'=4] {'gx_1'}, use_global_device_ids=true, to_apply=%add.2 | all-reduce | flops 2 | bytes 16
  23.4 0.6 reduce_sum.80
  24.0 1.4 dynamic-update-slice.2
  25.4 1.2 dynamic-slice.3
  26.6 10.5 %all-reduce.3 = f32[4]{0:T(128)S(1)} all-reduce(f32[4]{0:T(128)S(1)} %dynamic-update-slice.2), channel_id=1, replica_groups=mesh['gx_0'=4,'gx_1'=2,'gy_0'=4,'gy_1'=4] {'gy_0'}, use_global_device_ids=true, to_apply=%add.3 | all-reduce | flops 4 | bytes 32
  37.1 0.6 reduce_sum.81
  37.7 1.4 dynamic-update-slice.3
  39.1 10.7 %all-reduce.4 = f32[4]{0:T(128)S(1)} all-reduce(f32[4]{0:T(128)S(1)} %dynamic-update-slice.3), channel_id=1, replica_groups=mesh['gx_0'=4,'gx_1'=2,'gy_0'=4,'gy_1'=4] {'gy_1'}, use_global_device_ids=true, to_apply=%add.4 | all-reduce | flops 4 | bytes 32
  49.8 0.6 reduce_sum.82
  51.8 0.7 fusion.11
  52.5 1.4 scatter_custom_fusion
  54.0 0.0 copy-done
  54.0 1.9 %gather_fusion.1 = s32[256]{0:T(256)S(1)} fusion(s32[256]{0:T(256)S(1)} %bitcast.51, s32[1024]{0:T(1024)S(1)} %pad_clamp_fusion.1), kind=kCustom, calls=%fused_computation.2.clone | custom fusion | bytes 3072 | tf_op jit(solution)/shard_map/jit(take_along_axis)/gather | solution.py:58
  55.9 2.0 %gather_fusion = s32[256]{0:T(256)S(1)} fusion(s32[256]{0:T(256)} %bitcast.52, s32[1024]{0:T(1024)S(1)} %pad_clamp_fusion.1), kind=kCustom, calls=%fused_computation.clone | custom fusion | bytes 3072 | tf_op jit(solution)/shard_map/jit(take_along_axis)/gather | solution.py:57
  57.9 7.0 %all-gather.1 = f32[4,1,256]{2,1,0:T(1,128)S(1)} all-gather(f32[1,1,256]{2,1,0:T(1,128)S(1)} %multiply_bitcast_fusion), channel_id=1, replica_groups=mesh['gx_0'=4,'gx_1'=2,'gy_0'=4,'gy_1'=4] {'gy_0'}, dimensions={0}, use_global_device_ids=true | all-gather | bytes 5120 | tf_op jit(solution)/shard_map/all_gather | solution.py:16
  65.0 7.0 %all-gather.2 = f32[4,1,256]{2,1,0:T(1,128)S(1)} all-gather(f32[1,1,256]{2,1,0:T(1,128)S(1)} %bitcast.71), channel_id=2, replica_groups=mesh['gx_0'=4,'gx_1'=2,'gy_0'=4,'gy_1'=4] {'gy_1'}, dimensions={0}, use_global_device_ids=true | all-gather | bytes 5120 | tf_op jit(solution)/shard_map/all_gather | solution.py:16
  72.0 0.1 copy.23
  72.1 7.9 %gather_fusion.3 = f32[256,4096]{1,0:T(8,128)} fusion(f32[256,4096]{1,0:T(8,128)} %bitcast.53, s32[1024]{0:T(1024)S(1)} %pad_clamp_fusion), kind=kCustom, calls=%fused_computation.3.clone | custom fusion | bytes 8389632 | tf_op jit(solution)/shard_map/jit(take_along_axis)/gather | solution.py:55
  80.0 7.8 %gather_fusion.2 = f32[256,4096]{1,0:T(8,128)} fusion(f32[256,4096]{1,0:T(8,128)} %bitcast.54, s32[1024]{0:T(1024)S(1)} %pad_clamp_fusion), kind=kCustom, calls=%fused_computation.1.clone | custom fusion | bytes 8389632 | tf_op jit(solution)/shard_map/jit(take_along_axis)/gather | solution.py:56
  87.8 6.4 %fusion.8 = (f32[256]{0:T(256)S(1)}, f32[1,256,4096]{2,1,0:T(8,128)}) fusion(f32[256,4096]{1,0:T(8,128)} %gather_fusion.3, f32[256,4096]{1,0:T(8,128)} %gather_fusion.2, f32[256]{0:T(256)S(1)} %bitcast.65, f32[256]{0:T(256)S(1)} %bitcast.64, pred[256]{0:T(512)(128)(4,1)S(1)} %get-tuple-element.7, f32[]{:T(128)S(6)} %div.14), kind=kLoop, calls=%fused_computation.15 | loop fusion | flops 16776960 | bytes 12586244 | tf_op jit(solution)/shard_map/reduce_sum | solution.py:45
  94.2 0.1 copy.22
  94.3 5.6 %concatenate.7 = f32[1,256,4098]{2,1,0:T(8,128)} concatenate(f32[1,256,4096]{2,1,0:T(8,128)} %get-tuple-element.12, f32[1,256,1]{2,1,0:T(8,128)S(1)} %copy.22, f32[1,256,1]{2,1,0:T(8,128)S(1)} %copy.23), dimensions={2} | concatenate | bytes 8392704 | tf_op jit(solution)/shard_map/concatenate | solution.py:22
  99.9 6.7 %copy.24 = f32[1,256,4098]{2,0,1:T(1,128)S(1)} copy(f32[1,256,4098]{2,1,0:T(8,128)} %concatenate.7) | data formatting | bytes 8392704 | tf_op jit(solution)/shard_map/concatenate | solution.py:22
  106.6 49.0 %all_to_all.12 = f32[1,256,4098]{2,0,1:T(1,128)S(1)} all-to-all(f32[1,256,4098]{2,0,1:T(1,128)S(1)} %copy.24), channel_id=1, replica_groups=mesh['gx_0'=4,'gx_1'=2,'gy_0'=4,'gy_1'=4] {'gy_0','gy_1'}, dimensions={1} | all-to-all | bytes 8392704 | tf_op jit(solution)/shard_map/all_to_all | solution.py:24
  155.5 0.3 copy.25
  155.8 0.8 slice_reduce_fusion
  156.7 2.5 %slice.24 = f32[16,16,4096]{2,1,0:T(8,128)} slice(f32[16,16,4098]{2,1,0:T(8,128)S(1)} %bitcast.56), slice={[0:16], [0:16], [0:4096]} | slice | bytes 8388608 | tf_op jit(solution)/shard_map/slice | solution.py:29
  (17 shorter events, 0.1 us)
Async XLA Ops:
  0.6 53.3 %copy-start = (s32[1,256]{1,0:T(1,128)S(1)}, s32[1,256]{1,0:T(1,128)}, u32[]{:S(2)}) copy-start(s32[1,256]{1,0:T(1,128)} %param.12) | copy-start | bytes 3076
